TPU v7x, 8 devices: a whole 2x2x1 slice. The times are simulated.
8 devices in a mesh: dp: 1 (over z), tp: 8 (over y, x, core).
Axes of the slice: x: 2, y: 2, z: 1, core: 2. Of those that a mesh axis runs over, the one named last changes fastest.
Arguments:
- resid_in: bfloat16 [128, 8192], P('dp')
- positions: int32 [128], P('dp')
- k_cache: bfloat16 [128, 128, 8, 128], P('dp', None, 'tp')
- v_cache: bfloat16 [128, 128, 8, 128], P('dp', None, 'tp')
- gain_attn: bfloat16 [8192], replicated
- w_query: bfloat16 [8192, 8192], P(None, 'tp')
- w_key: bfloat16 [8192, 1024], P(None, 'tp')
- w_value: bfloat16 [8192, 1024], P(None, 'tp')
- w_out: bfloat16 [8192, 8192], P('tp')
- gain_mlp: bfloat16 [8192], replicated
- w_gate: bfloat16 [8192, 22016], P(None, 'tp')
- w_up: bfloat16 [8192, 22016], P(None, 'tp')
- w_down: bfloat16 [22016, 8192], P('tp')
Outputs:
- output 1: bfloat16 [128, 8192], P('dp')
- output 2: bfloat16 [128, 128, 8, 128], P('dp', None, 'tp')
- output 3: bfloat16 [128, 128, 8, 128], P('dp', None, 'tp')
All inputs are finite; a program needn't handle non-finite values.
Results may differ from a plain program's by a relative error of at most 0.010786.
Values sent between devices are 32-bit elements.
A program may use at most 1 GiB of HBM per device.

v0:
```python
import math
import jax
import jax.numpy as jnp
from jax import lax
from jax.experimental import pallas as pl
from jax.experimental.pallas import tpu as pltpu
from jax.sharding import PartitionSpec as P

EPS = 1e-5
ROPE_THETA = 500000.0
ROPE_FACTOR = 8.0
LOW_FACTOR = 1.0
HIGH_FACTOR = 4.0
ORIG_CTX = 8192.0


def rope_freqs(head_dim):
    half_dim = head_dim // 2
    exponents = (jnp.arange(head_dim, dtype=jnp.int32) % half_dim).astype(jnp.float32) * (2.0 / head_dim)
    inv_freq = 1.0 / jnp.power(ROPE_THETA, exponents)
    wavelen = (2.0 * math.pi) / inv_freq
    smooth = (ORIG_CTX / wavelen - LOW_FACTOR) / (HIGH_FACTOR - LOW_FACTOR)
    blended = (1.0 - smooth) * inv_freq / ROPE_FACTOR + smooth * inv_freq
    inv_freq = jnp.where(wavelen < ORIG_CTX / HIGH_FACTOR, inv_freq,
                         jnp.where(wavelen > ORIG_CTX / LOW_FACTOR, inv_freq / ROPE_FACTOR, blended))
    return inv_freq[None, :]


def front_kernel(pos_ref, resid_hbm, gain_ref, pos_row_ref, freq_ref, w_query_hbm, w_key_hbm, w_value_hbm,
                 k_in_hbm, v_in_hbm, attn_ref, k_out_hbm, v_out_hbm,
                 w_buf, acc, k_buf, v_buf, q_rows, o_rows, k_new, v_new, gain_f, cos_ref, sin_ref, resid_ref,
                 resid_sem, w_sem, cache_sem, out_sem):
    n_seqs, width = resid_ref.shape
    depth, q_width = w_buf.shape[1], w_query_hbm.shape[1]
    head_dim = k_new.shape[1]
    group_size = q_width // head_dim
    n_block = n_seqs // SEQ_BLOCK

    def w_copies(c):
        span = pl.ds(pl.multiple_of(c * depth, depth), depth)
        copies = []
        for i, (src, lo, size) in enumerate(((w_query_hbm, 0, q_width), (w_key_hbm, q_width, head_dim),
                                             (w_value_hbm, q_width + head_dim, head_dim))):
            copies.append(pltpu.make_async_copy(src.at[span], w_buf.at[c, :, pl.ds(lo, size)], w_sem.at[i, c]))
        return copies

    def block(b):
        return pl.ds(pl.multiple_of(b * SEQ_BLOCK, SEQ_BLOCK), SEQ_BLOCK)

    def in_copies(b):
        return (pltpu.make_async_copy(k_in_hbm.at[block(b)], k_buf.at[block(b)], cache_sem.at[0, b]),
                pltpu.make_async_copy(v_in_hbm.at[block(b)], v_buf.at[block(b)], cache_sem.at[1, b]))

    def out_copies(b):
        return (pltpu.make_async_copy(k_buf.at[block(b)], k_out_hbm.at[block(b)], out_sem.at[0, b]),
                pltpu.make_async_copy(v_buf.at[block(b)], v_out_hbm.at[block(b)], out_sem.at[1, b]))

    n_w = width // depth
    resid_copy = pltpu.make_async_copy(resid_hbm, resid_ref, resid_sem)
    resid_copy.start()
    for copy in w_copies(0):
        copy.start()
    gain_f[...] = gain_ref[...].astype(jnp.float32)

    def cols(c):
        return pl.ds(pl.multiple_of(c * depth, depth), depth)

    def add_squares(c, total):
        part = resid_ref[:, cols(c)].astype(jnp.float32)
        part = part * part
        for j in range(depth // 128):
            total = total + part[:, j * 128:(j + 1) * 128]
        return total

    acc[...] = jnp.zeros_like(acc)
    angles = (jnp.broadcast_to(pos_row_ref[...].astype(jnp.float32), (n_seqs, n_seqs)).T[:, :1]
              * freq_ref[...])
    cos_f = jnp.cos(angles)
    sin_f = jnp.sin(angles)
    sin_f = jnp.where(lax.broadcasted_iota(jnp.int32, sin_f.shape, 1) < head_dim // 2, -sin_f, sin_f)
    cos_ref[...] = cos_f
    sin_ref[...] = sin_f
    resid_copy.wait()
    for c in range(1, W_AHEAD):
        for copy in w_copies(c):
            copy.start()
    squares = lax.fori_loop(0, n_w, add_squares, jnp.zeros((n_seqs, 128), jnp.float32))
    scale = lax.rsqrt(jnp.sum(squares, axis=-1, keepdims=True) * (1.0 / width) + EPS)
    per_step = n_block // (n_w // 2)

    def project(c, carry):
        rows_f = resid_ref[:, cols(c)].astype(jnp.float32) * scale
        normed = jnp.concatenate(
            [rows_f[:, j * 128:(j + 1) * 128] * gain_f[pl.ds(c * (depth // 128) + j, 1), :]
             for j in range(depth // 128)], axis=-1).astype(jnp.bfloat16)
        for copy in w_copies(c):
            copy.wait()

        @pl.when(c + W_AHEAD < n_w)
        def _():
            for copy in w_copies(c + W_AHEAD):
                copy.start()

        @pl.when(c >= n_w // 2)
        def _():
            for i in range(per_step):
                for copy in in_copies((c - n_w // 2) * per_step + i):
                    copy.start()

        acc[...] += jnp.dot(normed, w_buf[c], preferred_element_type=jnp.float32)
        return carry

    lax.fori_loop(0, n_w, project, 0)

    def rotate(cols_f):
        values = cols_f.astype(jnp.bfloat16).astype(jnp.float32)
        turned = values * cos_ref[...] + pltpu.roll(values, head_dim // 2, 1) * sin_ref[...]
        return turned.astype(jnp.bfloat16).astype(jnp.float32)

    for j in range(group_size):
        q_rows[pl.ds(j, n_seqs, stride=group_size), :] = rotate(acc[:, j * head_dim:(j + 1) * head_dim])
    k_new[...] = rotate(acc[:, q_width:q_width + head_dim])
    v_new[...] = acc[:, q_width + head_dim:].astype(jnp.bfloat16).astype(jnp.float32)
    inv_sqrt = 1.0 / math.sqrt(head_dim)

    def attend(b, carry):
        for copy in in_copies(b):
            copy.wait()
        for i in range(SEQ_BLOCK):
            seq = b * SEQ_BLOCK + i
            pos = pos_ref[seq]
            base = pl.multiple_of(pos // 16 * 16, 16)
            hit = lax.broadcasted_iota(jnp.int32, (16, head_dim), 0) == pos - base
            for buf, new in ((k_buf, k_new), (v_buf, v_new)):
                old = buf[seq, pl.ds(base, 16), :].astype(jnp.float32)
                buf[seq, pl.ds(base, 16), :] = jnp.where(hit, new[pl.ds(seq, 1), :], old).astype(jnp.bfloat16)
        for copy in out_copies(b):
            copy.start()
        rows, probs = [], []
        for i in range(SEQ_BLOCK):
            seq = b * SEQ_BLOCK + i
            rows.append(pl.ds(pl.multiple_of(seq * group_size, group_size), group_size))
            query = q_rows[rows[i], :].astype(jnp.bfloat16)
            scores = lax.dot_general(query, k_buf[seq], (((1,), (1,)), ((), ())),
                                     preferred_element_type=jnp.float32) * inv_sqrt
            valid = lax.broadcasted_iota(jnp.int32, scores.shape, 1) <= pos_ref[seq]
            scores = jnp.where(valid, scores, -jnp.inf)
            exps = jnp.exp(scores - jnp.max(scores, axis=-1, keepdims=True))
            probs.append((exps / jnp.sum(exps, axis=-1, keepdims=True)).astype(jnp.bfloat16))
        for i in range(SEQ_BLOCK):
            o_rows[rows[i], :] = jnp.dot(probs[i], v_buf[b * SEQ_BLOCK + i], preferred_element_type=jnp.float32)
        return carry

    lax.fori_loop(0, n_block, attend, 0)
    for j in range(group_size):
        attn_ref[:, j * head_dim:(j + 1) * head_dim] = (
            o_rows[pl.ds(j, n_seqs, stride=group_size), :].astype(jnp.bfloat16))
    for b in range(n_block):
        for copy in out_copies(b):
            copy.wait()


SEQ_BLOCK = 32
FRONT_DEPTH = 2048
W_AHEAD = 2


def layer_front(resid_in, positions, k_cache, v_cache, gain_attn, w_query, w_key, w_value):
    n_seqs, width = resid_in.shape
    cache_len, head_dim = k_cache.shape[1], k_cache.shape[3]
    q_width = w_query.shape[1]
    f32, bf16 = jnp.float32, jnp.bfloat16
    vmem = pl.BlockSpec(memory_space=pltpu.VMEM)
    hbm = pl.BlockSpec(memory_space=pl.ANY)
    dma = pltpu.SemaphoreType.DMA
    n_w, n_block = width // FRONT_DEPTH, n_seqs // SEQ_BLOCK
    flat = (n_seqs, cache_len, head_dim)
    attn_out, k_out, v_out = pl.pallas_call(
        front_kernel,
        out_shape=(jax.ShapeDtypeStruct((n_seqs, q_width), bf16),
                   jax.ShapeDtypeStruct(flat, bf16), jax.ShapeDtypeStruct(flat, bf16)),
        in_specs=[pl.BlockSpec(memory_space=pltpu.SMEM), hbm, vmem, vmem, vmem, hbm, hbm, hbm, hbm, hbm],
        out_specs=(vmem, hbm, hbm),
        scratch_shapes=[
            pltpu.VMEM((n_w, FRONT_DEPTH, q_width + 2 * head_dim), bf16),
            pltpu.VMEM((n_seqs, q_width + 2 * head_dim), f32),
            pltpu.VMEM(flat, bf16),
            pltpu.VMEM(flat, bf16),
            pltpu.VMEM((n_seqs * q_width // head_dim, head_dim), f32),
            pltpu.VMEM((n_seqs * q_width // head_dim, head_dim), f32),
            pltpu.VMEM((n_seqs, head_dim), f32),
            pltpu.VMEM((n_seqs, head_dim), f32),
            pltpu.VMEM((width // 128, 128), f32),
            pltpu.VMEM((n_seqs, head_dim), f32),
            pltpu.VMEM((n_seqs, head_dim), f32),
            pltpu.VMEM((n_seqs, width), bf16),
            dma(()),
            dma((3, n_w)),
            dma((2, n_block)),
            dma((2, n_block)),
        ],
        compiler_params=pltpu.CompilerParams(vmem_limit_bytes=55050240),
        name='layer_front',
    )(positions, resid_in, pltpu.with_memory_space_constraint(gain_attn.reshape(width // 128, 128), pltpu.HBM),
      pltpu.with_memory_space_constraint(positions[None, :], pltpu.HBM),
      rope_freqs(head_dim), w_query, w_key, w_value,
      k_cache.reshape(flat), v_cache.reshape(flat))
    return attn_out, k_out.reshape(k_cache.shape), v_out.reshape(v_cache.shape)


N_CHUNK = 16
N_SLOT = 11
T_ROWS = 1024
MESH = pl.DeviceIdType.MESH


def tail_kernel(attn_ref, resid_hbm, gain_ref, w_out_hbm, gate_t_hbm, up_t_hbm, w_down_hbm, out_ref,
                part, from_core, from_1, from_2, gathered, mid, sq_sum, resid_own, gain_f,
                gate_acc, up_acc, gate_acc_t, up_acc_t, turned, hidden, ring,
                resid_sem, out_sem, ring_sem, rs_send, rs_recv, ag_send, ag_recv):
    n_chunk, chunk = N_CHUNK, part.shape[-1]
    half = chunk // 2
    rows = mid.shape[1]
    me = lax.axis_index('tp')
    k = me % 2
    x = (me // 2) % 2
    y = me // 4
    nk, nx, ny = 1 - k, 1 - x, 1 - y
    core_nbr = {'tp': me + 1 - 2 * k}
    x_nbr = {'tp': me + 2 - 4 * x}
    y_nbr = {'tp': me + 4 - 8 * y}

    def cols(c):
        return pl.ds(pl.multiple_of(c * chunk, chunk), chunk)

    depth_out = w_out_hbm.shape[0]
    first_mlp = n_chunk // 2
    first_down = first_mlp + 2 * n_chunk

    def out_slot(c):
        return c // 2, pl.ds(pl.multiple_of((c % 2) * depth_out, depth_out), depth_out)

    def out_copy(c):
        slot, span = out_slot(c)
        return pltpu.make_async_copy(w_out_hbm.at[:, cols(c)], ring.at[slot, span], out_sem.at[c])

    def ring_copy(src, c, j):
        slot = j % N_SLOT
        return pltpu.make_async_copy(src.at[:, cols(c)], ring.at[slot], ring_sem.at[slot])

    def gate_copy(c):
        return ring_copy(gate_t_hbm, c, first_mlp + 2 * c)

    def up_copy(c):
        return ring_copy(up_t_hbm, c, first_mlp + 2 * c + 1)

    def down_copy(c):
        return ring_copy(w_down_hbm, c, first_down + c)

    def start_load(j):
        m = j - first_mlp

        @pl.when(j < first_down)
        def _():
            @pl.when(m % 2 == 0)
            def _():
                gate_copy(m // 2).start()

            @pl.when(m % 2 == 1)
            def _():
                up_copy(m // 2).start()

        @pl.when(jnp.logical_and(j >= first_down, j < first_down + n_chunk))
        def _():
            down_copy(j - first_down).start()

    row0 = pl.multiple_of(64 * k + 32 * x + 16 * y, 16)
    resid_copy = pltpu.make_async_copy(resid_hbm.at[pl.ds(row0, rows)], resid_own, resid_sem)
    out_copy(0).start()

    barrier = pltpu.get_barrier_semaphore()
    for nbr in (core_nbr, x_nbr, y_nbr):
        pl.semaphore_signal(barrier, inc=1, device_id=nbr, device_id_type=MESH)

    def remote(src, dst, sems, ch, c, nbr):
        return pltpu.make_async_remote_copy(src_ref=src, dst_ref=dst, send_sem=sems[0].at[c],
                                            recv_sem=sems[1].at[ch, c], device_id=nbr, device_id_type=MESH)

    def wait_bytes(ref, sem):
        pltpu.make_async_copy(ref, ref, sem).wait()

    def wait_sent(sems, c):
        wait_bytes(mid.at[pl.ds(0, 7)], sems[0].at[c])

    rs = (rs_send, rs_recv)
    ag = (ag_send, ag_recv)
    left, right = pl.ds(0, half), pl.ds(half, half)

    def rs_core(c):
        return remote(part.at[c, nk], from_core.at[c], rs, 0, c, core_nbr)

    def rs_x1(c):
        return remote(part.at[c, k, nx, :, :, left], from_1.at[c, 0], rs, 1, c, x_nbr)

    def rs_y1(c):
        return remote(part.at[c, k, :, ny, :, right], from_1.at[c, 1], rs, 1, c, y_nbr)

    def rs_y2(c):
        return remote(part.at[c, k, x, ny, :, left], from_2.at[c, 0], rs, 2, c, y_nbr)

    def rs_x2(c):
        return remote(part.at[c, k, nx, y, :, right], from_2.at[c, 1], rs, 2, c, x_nbr)

    def ag_x(c):
        blk = gathered.at[c, k, x, y]
        return remote(blk, blk, ag, 0, c, x_nbr)

    def ag_y(c):
        blk = gathered.at[c, k, x, y]
        return remote(blk, blk, ag, 0, c, y_nbr)

    def ag_fwd_y(c):
        blk = gathered.at[c, k, nx, y, :, right]
        return remote(blk, blk, ag, 1, c, y_nbr)

    def ag_fwd_x(c):
        blk = gathered.at[c, k, x, ny, :, left]
        return remote(blk, blk, ag, 1, c, x_nbr)

    def ag_core(c):
        blk = gathered.at[c, k]
        return remote(blk, blk, ag, 2, c, core_nbr)

    def stage(s, lag, fn):
        c = s - lag

        @pl.when(jnp.logical_and(c >= 0, c < n_chunk))
        def _():
            fn(c)

    def rs_stage1(c):
        rs_core(c).wait_recv()
        part[c, k] = part[c, k] + from_core[c]
        rs_x1(c).start()
        rs_y1(c).start()

    def rs_stage2(c):
        wait_bytes(from_1.at[c], rs_recv.at[1, c])
        part[c, k, x, :, :, left] = part[c, k, x, :, :, left] + from_1[c, 0]
        part[c, k, :, y, :, right] = part[c, k, :, y, :, right] + from_1[c, 1]
        rs_y2(c).start()
        rs_x2(c).start()

    def rs_stage3(c):
        wait_bytes(from_2.at[c], rs_recv.at[2, c])
        total = jnp.concatenate([part[c, k, x, y, :, left] + from_2[c, 0],
                                 part[c, k, x, y, :, right] + from_2[c, 1]], axis=-1)
        wait_sent(rs, c)
        return total

    def ag_stage1(c):
        wait_bytes(from_1.at[c], ag_recv.at[0, c])
        ag_fwd_y(c).start()
        ag_fwd_x(c).start()

    def ag_stage2(c):
        wait_bytes(from_2.at[c], ag_recv.at[1, c])
        ag_core(c).start()

    def ag_stage3(c):
        ag_core(c).wait_recv()
        block = gathered[c].reshape(8 * rows, chunk)
        wait_sent(ag, c)
        return block

    gain_f[...] = gain_ref[...].astype(jnp.float32)
    sq_sum[...] = jnp.zeros_like(sq_sum)
    gate_acc[...] = jnp.zeros_like(gate_acc)
    up_acc[...] = jnp.zeros_like(up_acc)
    gate_acc_t[...] = jnp.zeros_like(gate_acc_t)
    up_acc_t[...] = jnp.zeros_like(up_acc_t)
    for c in range(1, OUT_AHEAD):
        out_copy(c).start()
    resid_copy.start()
    pl.semaphore_wait(barrier, 3)

    def proj(c):
        out_copy(c).wait()
        slot, span = out_slot(c)
        res = jnp.dot(attn_ref[...], ring[slot, span], preferred_element_type=jnp.float32)
        part[c] = res.reshape(part.shape[1:])
        rs_core(c).start()

        @pl.when(c + OUT_AHEAD < n_chunk)
        def _():
            out_copy(c + OUT_AHEAD).start()

        ahead = first_mlp + c - LOAD_LAG

        @pl.when(jnp.logical_and(c >= LOAD_LAG, ahead < N_SLOT))
        def _():
            start_load(ahead)

        @pl.when(c % 2 == 1)
        def _():
            start_load(c // 2 + N_SLOT)

    def finish_mid(c):
        @pl.when(c == 0)
        def _():
            resid_copy.wait()

        total = rs_stage3(c)
        x1 = (resid_own[:, cols(c)].astype(jnp.float32) + total).astype(jnp.bfloat16).astype(jnp.float32)
        mid[c] = x1
        sq_sum[...] += x1 * x1

    def rs_body(s, carry):
        stage(s, 0, proj)
        stage(s, RS1_LAG[0], rs_stage1)
        stage(s, RS1_LAG[1], rs_stage2)
        stage(s, RS1_LAG[2], finish_mid)
        return carry

    lax.fori_loop(0, n_chunk + RS1_LAG[2], rs_body, 0)

    mean_sq = jnp.sum(sq_sum[...], axis=-1, keepdims=True) * (1.0 / (n_chunk * chunk))
    scale = lax.rsqrt(mean_sq + EPS)

    def send_normed(c):
        gain = jnp.concatenate([gain_f[pl.ds(c * (chunk // 128) + j, 1), :] for j in range(chunk // 128)], axis=-1)
        normed = (mid[c] * scale * gain).astype(jnp.bfloat16)
        gathered[c, k, x, y] = normed.astype(jnp.float32)
        ag_x(c).start()
        ag_y(c).start()

    def gate_up(c):
        block = ag_stage3(c).astype(jnp.bfloat16)
        gate_copy(c).wait()
        up_copy(c).wait()
        first = first_mlp + 2 * c
        accs = ((gate_acc, gate_acc_t), (up_acc, up_acc_t))
        for i, (acc, acc_t) in enumerate(accs):
            slot = (first + i) % N_SLOT
            turned[i] = ring[slot, pl.ds(T_ROWS, acc_t.shape[1])].T
            acc[...] += lax.dot_general(ring[slot, pl.ds(0, T_ROWS)], block, (((1,), (1,)), ((), ())),
                                        preferred_element_type=jnp.float32)
        for i, (acc, acc_t) in enumerate(accs):
            acc_t[...] += jnp.dot(block, turned[i], preferred_element_type=jnp.float32)
        for i in range(2):
            start_load(first + i + N_SLOT)

    def ag_body(s, carry):
        stage(s, 0, send_normed)
        stage(s, AG1_LAG[0], ag_stage1)
        stage(s, AG1_LAG[1], ag_stage2)
        stage(s, AG1_LAG[2], gate_up)
        return carry

    lax.fori_loop(0, n_chunk + AG1_LAG[2], ag_body, 0)

    def act(gate, up):
        gate = gate.astype(jnp.bfloat16).astype(jnp.float32)
        up = up.astype(jnp.bfloat16).astype(jnp.float32)
        return jax.nn.silu(gate) * up

    for lo in range(0, T_ROWS, 128):
        span = slice(lo, lo + 128)
        hidden[:, span] = act(gate_acc[span, :], up_acc[span, :]).T.astype(jnp.bfloat16)
    hidden[:, T_ROWS:] = act(gate_acc_t[...], up_acc_t[...]).astype(jnp.bfloat16)

    def down(c):
        down_copy(c).wait()
        j = first_down + c
        res = jnp.dot(hidden[...], ring[j % N_SLOT], preferred_element_type=jnp.float32)
        part[c] = res.reshape(part.shape[1:])
        rs_core(c).start()
        start_load(j + N_SLOT)

    def finish_out(c):
        total = rs_stage3(c)
        gathered[c, k, x, y] = (mid[c] + total).astype(jnp.bfloat16).astype(jnp.float32)
        ag_x(c).start()
        ag_y(c).start()

    def store_out(c):
        out_ref[:, cols(c)] = ag_stage3(c).astype(jnp.bfloat16)

    base = RS2_LAG[2]

    def down_body(s, carry):
        stage(s, 0, down)
        stage(s, RS2_LAG[0], rs_stage1)
        stage(s, RS2_LAG[1], rs_stage2)
        stage(s, base, finish_out)
        stage(s, base + AG2_LAG[0], ag_stage1)
        stage(s, base + AG2_LAG[1], ag_stage2)
        stage(s, base + AG2_LAG[2], store_out)
        return carry

    lax.fori_loop(0, n_chunk + base + AG2_LAG[2], down_body, 0)


RS1_LAG = (2, 6, 10)
AG1_LAG = (2, 4, 5)
RS2_LAG = (2, 5, 8)
AG2_LAG = (2, 4, 5)
OUT_AHEAD = 4
LOAD_LAG = 4


def layer_tail(attn_out, resid_in, gain_mlp, w_out, w_gate, w_up, w_down):
    n_rows, width = resid_in.shape
    ffn = w_gate.shape[1]
    chunk = width // N_CHUNK
    half = chunk // 2
    rows = n_rows // 8
    f32, bf16 = jnp.float32, jnp.bfloat16
    vmem = pl.BlockSpec(memory_space=pltpu.VMEM)
    hbm = pl.BlockSpec(memory_space=pl.ANY)
    dma = pltpu.SemaphoreType.DMA
    return pl.pallas_call(
        tail_kernel,
        out_shape=jax.ShapeDtypeStruct((n_rows, width), bf16),
        in_specs=[vmem, hbm, vmem, hbm, hbm, hbm, hbm],
        out_specs=vmem,
        scratch_shapes=[
            pltpu.VMEM((N_CHUNK, 2, 2, 2, rows, chunk), f32),
            pltpu.VMEM((N_CHUNK, 2, 2, rows, chunk), f32),
            pltpu.VMEM((N_CHUNK, 2, 2, rows, half), f32),
            pltpu.VMEM((N_CHUNK, 2, rows, half), f32),
            pltpu.VMEM((N_CHUNK, 2, 2, 2, rows, chunk), f32),
            pltpu.VMEM((N_CHUNK, rows, chunk), f32),
            pltpu.VMEM((rows, chunk), f32),
            pltpu.VMEM((rows, width), bf16),
            pltpu.VMEM((width // 128, 128), f32),
            pltpu.VMEM((T_ROWS, n_rows), f32),
            pltpu.VMEM((T_ROWS, n_rows), f32),
            pltpu.VMEM((n_rows, ffn - T_ROWS), f32),
            pltpu.VMEM((n_rows, ffn - T_ROWS), f32),
            pltpu.VMEM((2, chunk, ffn - T_ROWS), bf16),
            pltpu.VMEM((n_rows, ffn), bf16),
            pltpu.VMEM((N_SLOT, ffn, chunk), bf16),
            dma(()),
            dma((N_CHUNK,)),
            dma((N_SLOT,)),
            dma((N_CHUNK,)),
            dma((3, N_CHUNK)),
            dma((N_CHUNK,)),
            dma((3, N_CHUNK)),
        ],
        compiler_params=pltpu.CompilerParams(collective_id=0, has_side_effects=True,
                                             vmem_limit_bytes=53477376),
        name='layer_tail',
    )(attn_out, resid_in, gain_mlp.reshape(width // 128, 128), w_out, w_gate.T, w_up.T, w_down)


def solution(mesh):
    def layer_local(resid_in, positions, k_cache, v_cache, gain_attn, w_query, w_key, w_value,
                    w_out, gain_mlp, w_gate, w_up, w_down):
        attn_out, k_full, v_full = layer_front(resid_in, positions, k_cache, v_cache,
                                               gain_attn, w_query, w_key, w_value)
        resid_out = layer_tail(attn_out, resid_in, gain_mlp, w_out, w_gate, w_up, w_down)
        return resid_out, k_full, v_full

    row_spec = P('dp', None)
    cache_spec = P('dp', None, 'tp', None)
    col_spec = P(None, 'tp')
    split_rows = P('tp', None)
    return jax.shard_map(layer_local, mesh=mesh,
                         in_specs=(row_spec, P('dp'), cache_spec, cache_spec, P(), col_spec, col_spec,
                                   col_spec, split_rows, P(), col_spec, col_spec, split_rows),
                         out_specs=(row_spec, cache_spec, cache_spec), check_vma=False)
```

profile of v0, /device:TPU:0, one launch (start us, length us, event | category | flops | bytes accessed | tf_op | source)
XLA Modules:
  0.0 116.6 jit_solution(5774199888021198650)
XLA Ops:
  0.7 0.0 copy-start
  0.7 16.2 %layer_front.1 = (bf16[128,1024]{1,0:T(8,128)(2,1)S(1)}, bf16[128,128,128]{2,1,0:T(8,128)(2,1)}, bf16[128,128,128]{2,1,0:T(8,128)(2,1)}) custom-call(s32[128]{0:T(128)} %pos_ref.1, bf16[128,8192]{1,0:T(8,128)(2,1)} %resid_hbm.3, bf16[64,128]{1,0:T(8,128)(2,1)} %bitcast.18, s32[1,128]{1,0:T(1,128)} %bitcast.19, f32[1,128]{1,0:T(1,128)S(1)} %compare_select_fusion.1.freq_ref, ...), custom_call_target="tpu_custom_call" | custom-call | tf_op jit(solution)/shard_map/layer_front/pallas_call | solution.py:178
  16.9 0.0 copy-done
  16.9 98.4 %layer_tail.1 = bf16[128,8192]{1,0:T(8,128)(2,1)S(1)} custom-call(bf16[128,1024]{1,0:T(8,128)(2,1)S(1)} %get-tuple-element.6.attn_ref, bf16[128,8192]{1,0:T(8,128)(2,1)} %resid_hbm.3, bf16[64,128]{1,0:T(8,128)(2,1)S(1)} %bitcast.13, bf16[1024,8192]{1,0:T(8,128)(2,1)} %w_out_hbm.1, bf16[2752,8192]{1,0:T(8,128)(2,1)} %bitcast.14, bf16[2752,8192]{1,0:T(8,128)(2,1)} %bitcast.15, ...), custom_call_target="tpu_custom_call" | custom-call | tf_op jit(solution)/shard_map/layer_tail/pallas_call | solution.py:522
  115.3 1.3 %copy.19 = bf16[128,8192]{1,0:T(8,128)(2,1)} copy(bf16[128,8192]{1,0:T(8,128)(2,1)S(1)} %layer_tail.1) | data formatting | bytes 4194304
  (1 shorter events, 0.0 us)
Async XLA Ops:
  0.7 16.2 %copy-start = (bf16[8192]{0:T(1024)(128)(2,1)S(1)}, bf16[8192]{0:T(1024)(128)(2,1)}, u32[]{:S(2)}) copy-start(bf16[8192]{0:T(1024)(128)(2,1)} %param.22) | copy-start | bytes 49156
where the time goes:
time: 117 us
  Pallas kernels  115 us (98%)
  local copies, waits for them, and re-layouts  1.33 us (1%)
    pallas_call x1, Pallas kernels, layer_tail(): pl.pallas_call(tail_kernel, out_shape=jax.ShapeDtypeStruct((n_rows, width...  98.4 us
    pallas_call x1, Pallas kernels, layer_front(): pl.pallas_call(front_kernel, out_shape=(jax.ShapeDtypeStruct((n_seqs, q_w...  16.2 us

commit v1 on v0

--- a/solution.py
+++ b/solution.py
@@ -26,10 +26,10 @@
     return inv_freq[None, :]
 
 
-def front_kernel(pos_ref, resid_hbm, gain_ref, pos_row_ref, freq_ref, w_query_hbm, w_key_hbm, w_value_hbm,
+def front_kernel(pos_ref, resid_hbm, gain_hbm, pos_row_hbm, freq_ref, w_query_hbm, w_key_hbm, w_value_hbm,
                  k_in_hbm, v_in_hbm, attn_ref, k_out_hbm, v_out_hbm,
-                 w_buf, acc, k_buf, v_buf, q_rows, o_rows, k_new, v_new, gain_f, cos_ref, sin_ref, resid_ref,
-                 resid_sem, w_sem, cache_sem, out_sem):
+                 w_buf, acc, k_buf, v_buf, q_rows, o_rows, k_new, v_new, gain_f, cos_ref, sin_ref, resid_ref, gain_ref, pos_row_ref,
+                 small_sem, resid_sem, w_sem, cache_sem, out_sem):
     n_seqs, width = resid_ref.shape
     depth, q_width = w_buf.shape[1], w_query_hbm.shape[1]
     head_dim = k_new.shape[1]
@@ -56,16 +56,27 @@
                 pltpu.make_async_copy(v_buf.at[block(b)], v_out_hbm.at[block(b)], out_sem.at[1, b]))
 
     n_w = width // depth
-    resid_copy = pltpu.make_async_copy(resid_hbm, resid_ref, resid_sem)
-    resid_copy.start()
-    for copy in w_copies(0):
-        copy.start()
-    gain_f[...] = gain_ref[...].astype(jnp.float32)
-
     def cols(c):
         return pl.ds(pl.multiple_of(c * depth, depth), depth)
 
+    def resid_copy(c):
+        return pltpu.make_async_copy(resid_hbm.at[:, cols(c)], resid_ref.at[:, cols(c)], resid_sem.at[c])
+
+    small_copies = [pltpu.make_async_copy(pos_row_hbm, pos_row_ref, small_sem.at[0]),
+                    pltpu.make_async_copy(gain_hbm, gain_ref, small_sem.at[1])]
+    for copy in small_copies:
+        copy.start()
+    for c in range(n_w):
+        resid_copy(c).start()
+    for c in range(2):
+        for copy in w_copies(c):
+            copy.start()
+    for copy in small_copies:
+        copy.wait()
+    gain_f[...] = gain_ref[...].astype(jnp.float32)
+
     def add_squares(c, total):
+        resid_copy(c).wait()
         part = resid_ref[:, cols(c)].astype(jnp.float32)
         part = part * part
         for j in range(depth // 128):
@@ -80,11 +91,10 @@
     sin_f = jnp.where(lax.broadcasted_iota(jnp.int32, sin_f.shape, 1) < head_dim // 2, -sin_f, sin_f)
     cos_ref[...] = cos_f
     sin_ref[...] = sin_f
-    resid_copy.wait()
-    for c in range(1, W_AHEAD):
+    squares = lax.fori_loop(0, n_w, add_squares, jnp.zeros((n_seqs, 128), jnp.float32))
+    for c in range(2, W_AHEAD):
         for copy in w_copies(c):
             copy.start()
-    squares = lax.fori_loop(0, n_w, add_squares, jnp.zeros((n_seqs, 128), jnp.float32))
     scale = lax.rsqrt(jnp.sum(squares, axis=-1, keepdims=True) * (1.0 / width) + EPS)
     per_step = n_block // (n_w // 2)
 
@@ -161,8 +171,8 @@
 
 
 SEQ_BLOCK = 32
-FRONT_DEPTH = 2048
-W_AHEAD = 2
+FRONT_DEPTH = 1024
+W_AHEAD = 4
 
 
 def layer_front(resid_in, positions, k_cache, v_cache, gain_attn, w_query, w_key, w_value):
@@ -179,7 +189,7 @@
         front_kernel,
         out_shape=(jax.ShapeDtypeStruct((n_seqs, q_width), bf16),
                    jax.ShapeDtypeStruct(flat, bf16), jax.ShapeDtypeStruct(flat, bf16)),
-        in_specs=[pl.BlockSpec(memory_space=pltpu.SMEM), hbm, vmem, vmem, vmem, hbm, hbm, hbm, hbm, hbm],
+        in_specs=[pl.BlockSpec(memory_space=pltpu.SMEM), hbm, hbm, hbm, vmem, hbm, hbm, hbm, hbm, hbm],
         out_specs=(vmem, hbm, hbm),
         scratch_shapes=[
             pltpu.VMEM((n_w, FRONT_DEPTH, q_width + 2 * head_dim), bf16),
@@ -194,7 +204,10 @@
             pltpu.VMEM((n_seqs, head_dim), f32),
             pltpu.VMEM((n_seqs, head_dim), f32),
             pltpu.VMEM((n_seqs, width), bf16),
-            dma(()),
+            pltpu.VMEM((width // 128, 128), bf16),
+            pltpu.VMEM((1, n_seqs), jnp.int32),
+            dma((2,)),
+            dma((n_w,)),
             dma((3, n_w)),
             dma((2, n_block)),
             dma((2, n_block)),
@@ -229,6 +242,7 @@
     core_nbr = {'tp': me + 1 - 2 * k}
     x_nbr = {'tp': me + 2 - 4 * x}
     y_nbr = {'tp': me + 4 - 8 * y}
+    far_nbr = {'tp': me + 6 - 4 * x - 8 * y}
 
     def cols(c):
         return pl.ds(pl.multiple_of(c * chunk, chunk), chunk)
@@ -242,7 +256,7 @@
 
     def out_copy(c):
         slot, span = out_slot(c)
-        return pltpu.make_async_copy(w_out_hbm.at[:, cols(c)], ring.at[slot, span], out_sem.at[c])
+        return pltpu.make_async_copy(w_out_hbm.at[:, cols(c)], ring.at[slot, span], out_sem.at[c % OUT_AHEAD])
 
     def ring_copy(src, c, j):
         slot = j % N_SLOT
@@ -279,7 +293,7 @@
     out_copy(0).start()
 
     barrier = pltpu.get_barrier_semaphore()
-    for nbr in (core_nbr, x_nbr, y_nbr):
+    for nbr in (core_nbr, x_nbr, y_nbr, far_nbr):
         pl.semaphore_signal(barrier, inc=1, device_id=nbr, device_id_type=MESH)
 
     def remote(src, dst, sems, ch, c, nbr):
@@ -318,6 +332,10 @@
     def ag_y(c):
         blk = gathered.at[c, k, x, y]
         return remote(blk, blk, ag, 0, c, y_nbr)
+
+    def ag_far(c):
+        blk = gathered.at[c, k, x, y]
+        return remote(blk, blk, ag, 1, c, far_nbr)
 
     def ag_fwd_y(c):
         blk = gathered.at[c, k, nx, y, :, right]
@@ -382,7 +400,7 @@
     for c in range(1, OUT_AHEAD):
         out_copy(c).start()
     resid_copy.start()
-    pl.semaphore_wait(barrier, 3)
+    pl.semaphore_wait(barrier, 4)
 
     def proj(c):
         out_copy(c).wait()
@@ -483,6 +501,18 @@
         ag_x(c).start()
         ag_y(c).start()
 
+        @pl.when(c == n_chunk - 1)
+        def _():
+            ag_far(c).start()
+
+    def ag_stage1_out(c):
+        wait_bytes(from_1.at[c], ag_recv.at[0, c])
+
+        @pl.when(c < n_chunk - 1)
+        def _():
+            ag_fwd_y(c).start()
+            ag_fwd_x(c).start()
+
     def store_out(c):
         out_ref[:, cols(c)] = ag_stage3(c).astype(jnp.bfloat16)
 
@@ -493,7 +523,7 @@
         stage(s, RS2_LAG[0], rs_stage1)
         stage(s, RS2_LAG[1], rs_stage2)
         stage(s, base, finish_out)
-        stage(s, base + AG2_LAG[0], ag_stage1)
+        stage(s, base + AG2_LAG[0], ag_stage1_out)
         stage(s, base + AG2_LAG[1], ag_stage2)
         stage(s, base + AG2_LAG[2], store_out)
         return carry
@@ -542,7 +572,7 @@
             pltpu.VMEM((n_rows, ffn), bf16),
             pltpu.VMEM((N_SLOT, ffn, chunk), bf16),
             dma(()),
-            dma((N_CHUNK,)),
+            dma((OUT_AHEAD,)),
             dma((N_SLOT,)),
             dma((N_CHUNK,)),
             dma((3, N_CHUNK)),

time: 117 us -> 117 us (level)
  no operation moved by 1% of the time
where the time goes in v1:
time: 117 us
  Pallas kernels  115 us (98%)
  local copies, waits for them, and re-layouts  1.33 us (1%)
    pallas_call x1, Pallas kernels, layer_tail(): pl.pallas_call(tail_kernel, out_shape=jax.ShapeDtypeStruct((n_rows, width...  98.3 us
    pallas_call x1, Pallas kernels, layer_front(): pl.pallas_call(front_kernel, out_shape=(jax.ShapeDtypeStruct((n_seqs, q_w...  16.8 us

profile of v1, /device:TPU:0, one launch (start us, length us, event | category | flops | bytes accessed | tf_op | source)
XLA Modules:
  0.0 117.1 jit_solution(3663227622378406405)
XLA Ops:
  0.7 0.0 copy-start
  0.7 16.8 %layer_front.1 = (bf16[128,1024]{1,0:T(8,128)(2,1)S(1)}, bf16[128,128,128]{2,1,0:T(8,128)(2,1)}, bf16[128,128,128]{2,1,0:T(8,128)(2,1)}) custom-call(s32[128]{0:T(128)} %pos_ref.1, bf16[128,8192]{1,0:T(8,128)(2,1)} %resid_hbm.3, bf16[64,128]{1,0:T(8,128)(2,1)} %bitcast.18, s32[1,128]{1,0:T(1,128)} %bitcast.19, f32[1,128]{1,0:T(1,128)S(1)} %compare_select_fusion.1.freq_ref, ...), custom_call_target="tpu_custom_call" | custom-call | tf_op jit(solution)/shard_map/layer_front/pallas_call | solution.py:188
  17.5 0.0 copy-done
  17.5 98.3 %layer_tail.1 = bf16[128,8192]{1,0:T(8,128)(2,1)S(1)} custom-call(bf16[128,1024]{1,0:T(8,128)(2,1)S(1)} %get-tuple-element.6.attn_ref, bf16[128,8192]{1,0:T(8,128)(2,1)} %resid_hbm.3, bf16[64,128]{1,0:T(8,128)(2,1)S(1)} %bitcast.13, bf16[1024,8192]{1,0:T(8,128)(2,1)} %w_out_hbm.1, bf16[2752,8192]{1,0:T(8,128)(2,1)} %bitcast.14, bf16[2752,8192]{1,0:T(8,128)(2,1)} %bitcast.15, ...), custom_call_target="tpu_custom_call" | custom-call | tf_op jit(solution)/shard_map/layer_tail/pallas_call | solution.py:552
  115.8 1.3 %copy.19 = bf16[128,8192]{1,0:T(8,128)(2,1)} copy(bf16[128,8192]{1,0:T(8,128)(2,1)S(1)} %layer_tail.1) | data formatting | bytes 4194304
  (1 shorter events, 0.0 us)
Async XLA Ops:
  0.7 16.8 %copy-start = (bf16[8192]{0:T(1024)(128)(2,1)S(1)}, bf16[8192]{0:T(1024)(128)(2,1)}, u32[]{:S(2)}) copy-start(bf16[8192]{0:T(1024)(128)(2,1)} %param.22) | copy-start | bytes 49156

commit v2 on v0

--- a/solution.py
+++ b/solution.py
@@ -56,8 +56,13 @@
                 pltpu.make_async_copy(v_buf.at[block(b)], v_out_hbm.at[block(b)], out_sem.at[1, b]))
 
     n_w = width // depth
-    resid_copy = pltpu.make_async_copy(resid_hbm, resid_ref, resid_sem)
-    resid_copy.start()
+
+    def resid_copy(c):
+        span = pl.ds(pl.multiple_of(c * depth, depth), depth)
+        return pltpu.make_async_copy(resid_hbm.at[:, span], resid_ref.at[:, span], resid_sem.at[c])
+
+    for c in range(n_w):
+        resid_copy(c).start()
     for copy in w_copies(0):
         copy.start()
     gain_f[...] = gain_ref[...].astype(jnp.float32)
@@ -66,6 +71,7 @@
         return pl.ds(pl.multiple_of(c * depth, depth), depth)
 
     def add_squares(c, total):
+        resid_copy(c).wait()
         part = resid_ref[:, cols(c)].astype(jnp.float32)
         part = part * part
         for j in range(depth // 128):
@@ -80,7 +86,6 @@
     sin_f = jnp.where(lax.broadcasted_iota(jnp.int32, sin_f.shape, 1) < head_dim // 2, -sin_f, sin_f)
     cos_ref[...] = cos_f
     sin_ref[...] = sin_f
-    resid_copy.wait()
     for c in range(1, W_AHEAD):
         for copy in w_copies(c):
             copy.start()
@@ -194,7 +199,7 @@
             pltpu.VMEM((n_seqs, head_dim), f32),
             pltpu.VMEM((n_seqs, head_dim), f32),
             pltpu.VMEM((n_seqs, width), bf16),
-            dma(()),
+            dma((n_w,)),
             dma((3, n_w)),
             dma((2, n_block)),
             dma((2, n_block)),
@@ -229,6 +234,7 @@
     core_nbr = {'tp': me + 1 - 2 * k}
     x_nbr = {'tp': me + 2 - 4 * x}
     y_nbr = {'tp': me + 4 - 8 * y}
+    far_nbr = {'tp': me + 6 - 4 * x - 8 * y}
 
     def cols(c):
         return pl.ds(pl.multiple_of(c * chunk, chunk), chunk)
@@ -242,7 +248,7 @@
 
     def out_copy(c):
         slot, span = out_slot(c)
-        return pltpu.make_async_copy(w_out_hbm.at[:, cols(c)], ring.at[slot, span], out_sem.at[c])
+        return pltpu.make_async_copy(w_out_hbm.at[:, cols(c)], ring.at[slot, span], out_sem.at[c % OUT_AHEAD])
 
     def ring_copy(src, c, j):
         slot = j % N_SLOT
@@ -279,7 +285,7 @@
     out_copy(0).start()
 
     barrier = pltpu.get_barrier_semaphore()
-    for nbr in (core_nbr, x_nbr, y_nbr):
+    for nbr in (core_nbr, x_nbr, y_nbr, far_nbr):
         pl.semaphore_signal(barrier, inc=1, device_id=nbr, device_id_type=MESH)
 
     def remote(src, dst, sems, ch, c, nbr):
@@ -318,6 +324,10 @@
     def ag_y(c):
         blk = gathered.at[c, k, x, y]
         return remote(blk, blk, ag, 0, c, y_nbr)
+
+    def ag_far(c):
+        blk = gathered.at[c, k, x, y]
+        return remote(blk, blk, ag, 1, c, far_nbr)
 
     def ag_fwd_y(c):
         blk = gathered.at[c, k, nx, y, :, right]
@@ -382,7 +392,7 @@
     for c in range(1, OUT_AHEAD):
         out_copy(c).start()
     resid_copy.start()
-    pl.semaphore_wait(barrier, 3)
+    pl.semaphore_wait(barrier, 4)
 
     def proj(c):
         out_copy(c).wait()
@@ -483,6 +493,18 @@
         ag_x(c).start()
         ag_y(c).start()
 
+        @pl.when(c == n_chunk - 1)
+        def _():
+            ag_far(c).start()
+
+    def ag_stage1_out(c):
+        wait_bytes(from_1.at[c], ag_recv.at[0, c])
+
+        @pl.when(c < n_chunk - 1)
+        def _():
+            ag_fwd_y(c).start()
+            ag_fwd_x(c).start()
+
     def store_out(c):
         out_ref[:, cols(c)] = ag_stage3(c).astype(jnp.bfloat16)
 
@@ -493,7 +515,7 @@
         stage(s, RS2_LAG[0], rs_stage1)
         stage(s, RS2_LAG[1], rs_stage2)
         stage(s, base, finish_out)
-        stage(s, base + AG2_LAG[0], ag_stage1)
+        stage(s, base + AG2_LAG[0], ag_stage1_out)
         stage(s, base + AG2_LAG[1], ag_stage2)
         stage(s, base + AG2_LAG[2], store_out)
         return carry
@@ -542,7 +564,7 @@
             pltpu.VMEM((n_rows, ffn), bf16),
             pltpu.VMEM((N_SLOT, ffn, chunk), bf16),
             dma(()),
-            dma((N_CHUNK,)),
+            dma((OUT_AHEAD,)),
             dma((N_SLOT,)),
             dma((N_CHUNK,)),
             dma((3, N_CHUNK)),

time: 117 us -> 117 us (level)
  no operation moved by 1% of the time
where the time goes in v2:
time: 117 us
  Pallas kernels  115 us (98%)
  local copies, waits for them, and re-layouts  1.33 us (1%)
    pallas_call x1, Pallas kernels, layer_tail(): pl.pallas_call(tail_kernel, out_shape=jax.ShapeDtypeStruct((n_rows, width...  98.4 us
    pallas_call x1, Pallas kernels, layer_front(): pl.pallas_call(front_kernel, out_shape=(jax.ShapeDtypeStruct((n_seqs, q_w...  16.7 us

profile of v2, /device:TPU:0, one launch (start us, length us, event | category | flops | bytes accessed | tf_op | source)
XLA Modules:
  0.0 117.1 jit_solution(18214774296096749337)
XLA Ops:
  0.7 0.0 copy-start
  0.7 16.7 %layer_front.1 = (bf16[128,1024]{1,0:T(8,128)(2,1)S(1)}, bf16[128,128,128]{2,1,0:T(8,128)(2,1)}, bf16[128,128,128]{2,1,0:T(8,128)(2,1)}) custom-call(s32[128]{0:T(128)} %pos_ref.1, bf16[128,8192]{1,0:T(8,128)(2,1)} %resid_hbm.3, bf16[64,128]{1,0:T(8,128)(2,1)} %bitcast.18, s32[1,128]{1,0:T(1,128)} %bitcast.19, f32[1,128]{1,0:T(1,128)S(1)} %compare_select_fusion.1.freq_ref, ...), custom_call_target="tpu_custom_call" | custom-call | tf_op jit(solution)/shard_map/layer_front/pallas_call | solution.py:183
  17.4 0.0 copy-done
  17.4 98.4 %layer_tail.1 = bf16[128,8192]{1,0:T(8,128)(2,1)S(1)} custom-call(bf16[128,1024]{1,0:T(8,128)(2,1)S(1)} %get-tuple-element.6.attn_ref, bf16[128,8192]{1,0:T(8,128)(2,1)} %resid_hbm.3, bf16[64,128]{1,0:T(8,128)(2,1)S(1)} %bitcast.13, bf16[1024,8192]{1,0:T(8,128)(2,1)} %w_out_hbm.1, bf16[2752,8192]{1,0:T(8,128)(2,1)} %bitcast.14, bf16[2752,8192]{1,0:T(8,128)(2,1)} %bitcast.15, ...), custom_call_target="tpu_custom_call" | custom-call | tf_op jit(solution)/shard_map/layer_tail/pallas_call | solution.py:544
  115.8 1.3 %copy.19 = bf16[128,8192]{1,0:T(8,128)(2,1)} copy(bf16[128,8192]{1,0:T(8,128)(2,1)S(1)} %layer_tail.1) | data formatting | bytes 4194304
  (1 shorter events, 0.0 us)
Async XLA Ops:
  0.7 16.7 %copy-start = (bf16[8192]{0:T(1024)(128)(2,1)S(1)}, bf16[8192]{0:T(1024)(128)(2,1)}, u32[]{:S(2)}) copy-start(bf16[8192]{0:T(1024)(128)(2,1)} %param.22) | copy-start | bytes 49156
